TPU v7x, 32 devices: a whole 2x2x4 slice. The times are simulated.
32 devices in a mesh: dp: 8 (over y, x, core), tensor: 4 (over z).
Axes of the slice: x: 2, y: 2, z: 4, core: 2. Of those that a mesh axis runs over, the one named last changes fastest.
Arguments:
- features: bfloat16 [2048, 1024], P(('dp', 'tensor')), may hold values from -6 to 6
- click: int32 [2048], P(('dp', 'tensor')), may hold values 0 or 1
- convert: int32 [2048], P(('dp', 'tensor')), may hold values 0 or 1
- w1: bfloat16 [1024, 2, 4096], P('dp', None, 'tensor'), may hold values from -0.1875 to 0.1875
- b1: float32 [2, 4096], P(None, 'tensor'), may hold values from -4 to 4
- w2: bfloat16 [2, 4096], P(None, 'tensor'), may hold values from -0.1875 to 0.1875
Outputs:
- sample_loss: float32 [2048], P(('dp', 'tensor'))
- grad_features: bfloat16 [2048, 1024], P(('dp', 'tensor'))
- grad_w1: float32 [1024, 2, 4096], P('dp', None, 'tensor')
- grad_b1: float32 [2, 4096], P(None, 'tensor')
- grad_w2: float32 [2, 4096], P(None, 'tensor')
All inputs are finite; a program needn't handle non-finite values. No bound on the sum of `click` or of `convert` on one device may be relied on, other than what follows from the above.
Results may differ from a plain program's by a relative error of at most 0.025.
Values may be sent and summed in bfloat16 or wider, within the bound.
A program may use at most 64 MiB of HBM per device.

v0:
```python
import math
import jax
import jax.numpy as jnp
from jax import lax
from jax.sharding import PartitionSpec as P


def sample_loss_fn(logits, click, convert):
    first = logits[:, 0]
    second = logits[:, 1]
    label_y = click.astype(jnp.float32)
    label_z = (click * convert).astype(jnp.float32)
    rest = jnp.log(jax.nn.sigmoid(-first) + jax.nn.sigmoid(first) * jax.nn.sigmoid(-second))
    click_part = label_y * jax.nn.log_sigmoid(first) + (1.0 - label_y) * jax.nn.log_sigmoid(-first)
    both_part = (
        label_z * (jax.nn.log_sigmoid(first) + jax.nn.log_sigmoid(second)) + (1.0 - label_z) * rest
    )
    return -click_part - both_part


def loss_slope(logits, click, convert):
    losses, pullback = jax.vjp(lambda value: sample_loss_fn(value, click, convert), logits)
    return (losses, pullback(jnp.ones_like(losses))[0])


def local(features, click, convert, w1, b1, w2):
    own_count, width = features.shape
    local_units = w1.shape[2]
    total = own_count * lax.axis_size("dp") * lax.axis_size("tensor")
    scale = 1.0 / math.sqrt(total)
    group = lax.all_gather(features, "tensor", axis=0, tiled=True)
    group_count = group.shape[0]
    w2f = w2.astype(jnp.float32)
    full_weights = lax.all_gather(w1, "dp", axis=0, tiled=True)
    w_flat = full_weights.reshape(width, 2 * local_units)
    pre_flat = jnp.dot(group, w_flat, preferred_element_type=jnp.float32)
    pre = pre_flat.reshape(group_count, 2, local_units) + b1[None]
    hidden = jnp.maximum(pre, 0.0).astype(jnp.bfloat16)
    partial_logits = jnp.sum(hidden.astype(jnp.float32) * w2f[None], axis=2)
    logits = lax.psum(partial_logits, "tensor")
    labels = lax.all_gather(jnp.stack([click, convert], axis=1), "tensor", axis=0, tiled=True)
    losses_all, slope = loss_slope(logits, labels[:, 0], labels[:, 1])
    offset = lax.axis_index("tensor") * own_count
    losses = lax.dynamic_slice_in_dim(losses_all, offset, own_count, 0)
    dhidden = jnp.where(pre > 0.0, slope[:, :, None] * w2f[None], 0.0).astype(jnp.bfloat16)
    d_flat = dhidden.reshape(group_count, 2 * local_units)
    partial_rows = jnp.dot(d_flat, w_flat.T, preferred_element_type=jnp.float32)
    grad_features = lax.psum_scatter(
        partial_rows.astype(jnp.bfloat16), "tensor", scatter_dimension=0, tiled=True
    )
    grad_w1 = (
        lax.psum_scatter(
            jnp.dot(group.T, d_flat, preferred_element_type=jnp.float32).reshape(
                w1.shape[0] * lax.axis_size("dp"), 2, local_units
            ),
            "dp",
            scatter_dimension=0,
            tiled=True,
        )
        * scale
    )
    bias_term = jnp.sum(dhidden.astype(jnp.float32), axis=0)
    out_term = jnp.sum(slope[:, :, None] * hidden.astype(jnp.float32), axis=0)
    stacked = jnp.concatenate([bias_term, out_term], axis=0).reshape(4 * local_units)
    summed_share = lax.psum_scatter(stacked, "dp", scatter_dimension=0, tiled=True)
    summed = lax.all_gather(summed_share, "dp", axis=0, tiled=True).reshape(4, local_units)
    return (losses, grad_features, grad_w1, summed[0:2] * scale, summed[2:4] * scale)


def solution(mesh):
    placed = (
        P(("dp", "tensor"), None),
        P(("dp", "tensor")),
        P(("dp", "tensor")),
        P("dp", None, "tensor"),
        P(None, "tensor"),
        P(None, "tensor"),
    )
    return jax.shard_map(
        local,
        mesh=mesh,
        in_specs=placed,
        out_specs=(
            P(("dp", "tensor")),
            P(("dp", "tensor"), None),
            P("dp", None, "tensor"),
            P(None, "tensor"),
            P(None, "tensor"),
        ),
        check_vma=False,
    )
```

profile of v0, /device:TPU:0, one launch (start us, length us, event | category | flops | bytes accessed | tf_op | source)
XLA Modules:
  0.0 247.1 jit_solution(14040047813473934974)
XLA Ops:
  7.2 0.0 all-gather.4.cloned.1.call-start
  7.2 2.0 copy.19
  9.2 0.0 all-gather.4.cloned.1.call-update
  9.2 0.0 all-reduce.6.cloned.1.call-start
  9.2 0.7 convert_element_type.35
  9.9 0.7 add_bitcast_fusion
  10.6 12.6 %all-gather = s32[4,64,2]{1,2,0:T(2,128)S(1)} all-gather(s32[1,64,2]{1,2,0:T(2,128)S(1)} %add_bitcast_fusion), channel_id=1, replica_groups=mesh['dp'=8,'tensor'=4] {'tensor'}, dimensions={0}, use_global_device_ids=true | all-gather | bytes 2560 | tf_op jit(solution)/shard_map/all_gather | solution.py:41
  23.3 0.1 reshape.58
  23.3 15.0 %all_gather.13 = bf16[256,1024]{1,0:T(8,128)(2,1)S(1)} all-gather(bf16[64,1024]{1,0:T(8,128)(2,1)} %param.7), channel_id=1, replica_groups=mesh['dp'=8,'tensor'=4] {'tensor'}, dimensions={0}, use_global_device_ids=true | all-gather | bytes 655360 | tf_op jit(solution)/shard_map/all_gather | solution.py:31
  38.3 0.0 copy-start
  38.3 0.0 copy-start.2
  38.3 11.5 %all-gather.4.cloned.1.call-done = bf16[1024,2,1024]{2,0,1:T(8,128)(2,1)} async-done(((bf16[128,2,1024]{2,0,1:T(8,128)(2,1)}), bf16[1024,2,1024]{2,0,1:T(8,128)(2,1)}) %all-gather.4.cloned.1.call-update) | async-done | bytes 4194320 | tf_op jit(solution)/shard_map/all_gather | solution.py:34
  49.8 6.2 %copy.20 = bf16[1024,2,1024]{0,2,1:T(8,128)(2,1)} copy(bf16[1024,2,1024]{2,0,1:T(8,128)(2,1)} %all-gather.4.cloned.1.call-done) | data formatting | bytes 8388608 | tf_op jit(solution)/shard_map/all_gather | solution.py:34
  56.0 0.0 copy-done
  56.0 0.0 copy-done.2
  56.0 3.6 %fusion.2 = (f32[256,2]{0,1:T(2,128)S(1)}, f32[256,2,1024]{2,0,1:T(8,128)S(1)}) fusion(f32[2,1024]{1,0:T(2,128)S(1)} %convert_element_type.35, f32[2,1024]{1,0:T(2,128)S(1)} %copy-done.2, bf16[1024,2,1024]{0,2,1:T(8,128)(2,1)} %copy.20, bf16[256,1024]{1,0:T(8,128)(2,1)S(1)} %all_gather.13), kind=kOutput, calls=%fused_computation.4 | convolution fusion | flops 1076887040 | bytes 6834176 | tf_op jit(solution)/shard_map/dot_general | solution.py:36
  59.6 11.7 %psum.7 = f32[256,2]{0,1:T(2,128)S(1)} all-reduce(f32[256,2]{0,1:T(2,128)S(1)} %get-tuple-element.29), channel_id=1, replica_groups=mesh['dp'=8,'tensor'=4] {'tensor'}, use_global_device_ids=true, to_apply=%region_1.0 | all-reduce | flops 512 | bytes 4096 | tf_op jit(solution)/shard_map/psum | solution.py:40
  71.3 0.4 fusion.5
  71.7 0.8 convert_reduce_fusion
  72.5 0.0 copy-start.1
  72.5 0.5 copy.21
  73.1 0.5 copy-done.1
  73.6 4.5 %fusion.34 = f32[2048,1024]{1,0:T(8,128)} fusion(bf16[256,2048]{0,1:T(8,128)(2,1)S(1)} %bitcast.45, bf16[256,1024]{1,0:T(8,128)(2,1)S(1)} %copy-done.1), kind=kOutput, calls=%fused_computation.71 | convolution fusion | flops 1073741824 | bytes 9961472 | tf_op jit(solution)/shard_map/dot_general | solution.py:53
  78.0 13.4 %copy.22 = f32[1024,2,1024]{2,1,0:T(2,128)} copy(f32[1024,2,1024]{0,2,1:T(8,128)} %bitcast.44) | data formatting | bytes 16777216 | tf_op jit(solution)/shard_map/reshape | solution.py:53
  91.4 0.0 all-reduce.6.cloned.1.call-update
  91.4 0.0 copy-start.3
  91.4 0.0 reduce-scatter.2.cloned.1.call-start
  91.5 4.3 %fusion.4 = bf16[256,1024]{1,0:T(8,128)(2,1)} fusion(bf16[1024,2,1024]{2,0,1:T(8,128)(2,1)} %all-gather.4.cloned.1.call-done, f32[256,2]{0,1:T(2,128)S(1)} %pad_add_fusion, f32[2,1024]{1,0:T(2,128)S(1)} %convert_element_type.35, u8[256,1024]{1,0:T(8,128)(4,1)S(1)} %fusion.5), kind=kOutput, calls=%fused_computation.12 | convolution fusion | flops 1077673984 | bytes 4990976 | tf_op jit(solution)/shard_map/dot_general | solution.py:47
  95.8 0.0 reduce-scatter.2.cloned.1.call-update
  95.8 0.0 copy-done.3
  95.8 0.6 dynamic-slice
  97.7 24.1 %all-reduce.3 = f32[4096]{0:T(1024)S(1)} all-reduce(f32[4096]{0:T(1024)S(1)} %bitcast.46), channel_id=4, replica_groups=mesh['dp'=8,'tensor'=4] {'dp'}, use_global_device_ids=true, to_apply=%region_6.8.clone | all-reduce | flops 4096 | bytes 32768
  121.8 0.1 dynamic-slice.3
  121.9 9.1 %all-gather.1 = f32[8,1,512]{2,1,0:T(1,128)S(1)} all-gather(f32[1,1,512]{2,1,0:T(1,128)S(1)} %bitcast.47), channel_id=1, replica_groups=mesh['dp'=8,'tensor'=4] {'dp'}, dimensions={0}, use_global_device_ids=true | all-gather | bytes 18432 | tf_op jit(solution)/shard_map/all_gather | solution.py:66
  131.0 0.1 fusion.7
  131.1 0.6 mul.146
  131.7 0.6 mul.148
  132.3 0.6 dynamic_slice.3
  132.9 82.8 %all-reduce.6.cloned.1.call-done = f32[1024,2,1024]{2,1,0:T(2,128)} async-done(((f32[1024,2,1024]{2,1,0:T(2,128)}), f32[1024,2,1024]{2,1,0:T(2,128)}) %all-reduce.6.cloned.1.call-update) | async-done | bytes 8388624
  215.7 2.7 %dynamic-slice_multiply_fusion = f32[128,2,1024]{2,1,0:T(2,128)} fusion(f32[1024,2,1024]{2,1,0:T(2,128)} %all-reduce.6.cloned.1.call-done, u32[]{:T(128)S(6)} %multiply.1), kind=kLoop, calls=%fused_computation.13 | loop fusion | flops 262144 | bytes 2097156 | tf_op jit(solution)/shard_map/mul | solution.py:52
  218.4 22.1 %reduce-scatter.2.cloned.1.call-done = bf16[64,1024]{1,0:T(8,128)(2,1)} async-done(((bf16[256,1024]{1,0:T(8,128)(2,1)}), bf16[64,1024]{1,0:T(8,128)(2,1)}) %reduce-scatter.2.cloned.1.call-update) | async-done | bytes 131088 | tf_op jit(solution)/shard_map/reduce_scatter | solution.py:48
  (7 shorter events, 0.1 us)
Async XLA Ops:
  7.2 42.6 %all-gather.4.cloned.1.call-start = ((), (), s32[]{:S(2)}) async-start(), calls=%async_computation.1 | async-start | bytes 4718592 | tf_op jit(solution)/shard_map/all_gather | solution.py:34
  9.2 206.5 %all-reduce.6.cloned.1.call-start = ((), (), s32[]{:S(2)}) async-start(), calls=%async_computation.3 | async-start | bytes 16777216
  38.3 17.7 %copy-start = (bf16[256,1024]{1,0:T(8,128)(2,1)}, bf16[256,1024]{1,0:T(8,128)(2,1)S(1)}, u32[]{:S(2)}) copy-start(bf16[256,1024]{1,0:T(8,128)(2,1)S(1)} %all_gather.13) | copy-start | bytes 1572868
  38.3 17.7 %copy-start.2 = (f32[2,1024]{1,0:T(2,128)S(1)}, f32[2,1024]{1,0:T(2,128)}, u32[]{:S(2)}) copy-start(f32[2,1024]{1,0:T(2,128)} %param.11) | copy-start | bytes 24580
  72.5 1.0 copy-start.1
  91.4 4.4 %copy-start.3 = (u32[32]{0:T(128)S(1)}, u32[32]{0:T(128)}, u32[]{:S(2)}) copy-start(u32[32]{0:T(128)} %constant.32) | copy-start | bytes 388
  91.4 149.1 %reduce-scatter.2.cloned.1.call-start = ((), (), s32[]{:S(2)}) async-start(), calls=%async_computation.2 | async-start | bytes 655360 | tf_op jit(solution)/shard_map/reduce_scatter | solution.py:48
Sparse Core Ops, SparseCore 0:
  10.4 39.2 all-gather.3
  91.5 124.0 all-reduce.5
  218.5 21.9 reduce-scatter.1
where the time goes:
time: 248 us; the launch traced here: 247 us
  waiting for transfers between devices  116 us (47%)
  blocking collectives  72.5 us (29%)
  local copies, waits for them, and re-layouts  25.2 us (10%)
  between operations  15.1 us (6%)
  matrix products  12.3 us (5%)
  other arithmetic  5.38 us (2%)
    unnamed x4, waiting for transfers between devices  82.8 us
    unnamed x1, blocking collectives  24.1 us
    reduce_scatter x1, waiting for transfers between devices, local(): lax.psum_scatter(partial_rows.astype(jnp.bfloat16), 'tensor', scatter_dim...  22.1 us
    all_gather x1, blocking collectives, local(): group = lax.all_gather(features, 'tensor', axis=0, tiled=True)  15 us
    reshape x1, local copies, waits for them, and re-layouts, local(): jnp.dot(group.T, d_flat, preferred_element_type=jnp.float32)  13.4 us
    all_gather x1, blocking collectives, local(): lax.all_gather(jnp.stack([click, convert], axis=1), 'tensor', axis=0, til...  12.6 us
    psum x1, blocking collectives, local(): logits = lax.psum(partial_logits, 'tensor')  11.7 us
    all_gather x1, waiting for transfers between devices, local(): full_weights = lax.all_gather(w1, 'dp', axis=0, tiled=True)  11.5 us
  transfers between devices with their start and end apart: 3, of which 3 were waited for; matrix products, arithmetic and copies ran while one was open for 4% of the time, Pallas kernels for 0%

commit v1 on v0

--- a/solution.py
+++ b/solution.py
@@ -28,7 +28,14 @@
     local_units = w1.shape[2]
     total = own_count * lax.axis_size("dp") * lax.axis_size("tensor")
     scale = 1.0 / math.sqrt(total)
-    group = lax.all_gather(features, "tensor", axis=0, tiled=True)
+    ring = [features]
+    for hop in range(3):
+        ring.append(lax.ppermute(ring[-1], "tensor", [(dev, (dev + 1) % 4) for dev in range(4)]))
+    group = jnp.roll(
+        jnp.concatenate(ring[::-1], axis=0),
+        (lax.axis_index("tensor") + 1) * ring[0].shape[0],
+        axis=0,
+    )
     group_count = group.shape[0]
     w2f = w2.astype(jnp.float32)
     full_weights = lax.all_gather(w1, "dp", axis=0, tiled=True)

time: 248 us -> 178 us (0.72)
  waiting for transfers between devices: 116 us -> 75 us
  blocking collectives: 72.5 us -> 54.8 us
  local copies, waits for them, and re-layouts: 25.2 us -> 13.9 us
  starting transfers between devices: 0.12 us -> 3.23 us
    unnamed x4 -> x3, waiting for transfers between devices: 82.8 us -> 0.05 us
    reduce_scatter x0 -> x1, waiting for transfers between devices: none -> 29.5 us  [local(): lax.psum_scatter(jnp.dot(group.T, d_flat, preferred_element_type=jnp.floa...]
    all_gather x1 -> x0, blocking collectives: 15 us -> none  [local(): group = lax.all_gather(features, 'tensor', axis=0, tiled=True)]
    reshape x1 -> x0, local copies, waits for them, and re-layouts: 13.4 us -> none  [local(): jnp.dot(group.T, d_flat, preferred_element_type=jnp.float32)]
    ppermute x0 -> x3, waiting for transfers between devices: none -> 12.5 us  [local(): lax.ppermute(ring[-1], 'tensor', [(dev, (dev + 1) % 4) for dev in range(4)])]
    ppermute x0 -> x3, starting transfers between devices: none -> 3.11 us  [local(): lax.ppermute(ring[-1], 'tensor', [(dev, (dev + 1) % 4) for dev in range(4)])]
    unnamed x13 -> x23, local copies, waits for them, and re-layouts: 3.22 us -> 5.3 us
  transfers between devices with their start and end apart: 3 -> 6, of which waited for: 3 -> 5; matrix products, arithmetic and copies ran while one was open for 4% -> 6% of each run, Pallas kernels for 0% -> 0%
where the time goes in v1:
time: 178 us
  waiting for transfers between devices  75 us (42%)
  blocking collectives  54.8 us (31%)
  between operations  14.6 us (8%)
  local copies, waits for them, and re-layouts  13.9 us (8%)
  matrix products  12.4 us (7%)
  other arithmetic  3.97 us (2%)
  starting transfers between devices  3.23 us (2%)
    reduce_scatter x1, waiting for transfers between devices, local(): lax.psum_scatter(jnp.dot(group.T, d_flat, preferred_element_type=jnp.floa...  29.5 us
    unnamed x1, blocking collectives  22.7 us
    reduce_scatter x1, waiting for transfers between devices, local(): lax.psum_scatter(partial_rows.astype(jnp.bfloat16), 'tensor', scatter_dim...  21.6 us
    ppermute x3, waiting for transfers between devices, local(): lax.ppermute(ring[-1], 'tensor', [(dev, (dev + 1) % 4) for dev in range(4)])  12.5 us
    psum x1, blocking collectives, local(): logits = lax.psum(partial_logits, 'tensor')  11.7 us
    all_gather x1, blocking collectives, local(): lax.all_gather(jnp.stack([click, convert], axis=1), 'tensor', axis=0, til...  11.4 us
    all_gather x1, waiting for transfers between devices, local(): full_weights = lax.all_gather(w1, 'dp', axis=0, tiled=True)  11.3 us
    all_gather x1, blocking collectives, local(): lax.all_gather(summed_share, 'dp', axis=0, tiled=True)  9.05 us
  transfers between devices with their start and end apart: 6, of which 5 were waited for; matrix products, arithmetic and copies ran while one was open for 6% of the time, Pallas kernels for 0%

profile of v1, /device:TPU:0, one launch (start us, length us, event | category | flops | bytes accessed | tf_op | source)
XLA Modules:
  0.0 177.8 jit_solution(17604402186211711153)
XLA Ops:
  7.2 0.0 copy-start
  7.2 0.0 all-gather.4.cloned.1.call-start
  7.2 2.0 %copy.21 = bf16[128,2,1024]{2,0,1:T(8,128)(2,1)} copy(bf16[128,2,1024]{2,1,0:T(2,128)(2,1)} %param.10) | data formatting | bytes 1048576 | tf_op args[3]
  9.2 0.0 all-gather.4.cloned.1.call-update
  9.2 0.0 reduce-scatter.5.cloned.1.call-start
  9.3 3.1 %collective-permute-start = (bf16[64,1024]{1,0:T(8,128)(2,1)}, bf16[64,1024]{1,0:T(8,128)(2,1)S(1)}, u32[]{:S(2)}, u32[]{:S(2)}) collective-permute-start(bf16[64,1024]{1,0:T(8,128)(2,1)} %param.7), channel_id=1, source_target_pairs={{0,1},{1,2},{2,3},{3,0},{4,5},{5,6},{6,7},{7,4},{8,9},{9,10},{10,1... | collective-permute-start | bytes 393224 | tf_op jit(solution)/shard_map/ppermute | solution.py:33
  12.4 5.7 %collective-permute-done = bf16[64,1024]{1,0:T(8,128)(2,1)S(1)} collective-permute-done((bf16[64,1024]{1,0:T(8,128)(2,1)}, bf16[64,1024]{1,0:T(8,128)(2,1)S(1)}, u32[]{:S(2)}, u32[]{:S(2)}) %collective-permute-start) | collective-permute-done | bytes 131104 | tf_op jit(solution)/shard_map/ppermute | solution.py:33
  18.1 0.0 collective-permute-start.1
  18.1 0.7 convert_element_type.35
  18.8 0.7 add_bitcast_fusion
  19.5 11.4 %all-gather = s32[4,64,2]{1,2,0:T(2,128)S(1)} all-gather(s32[1,64,2]{1,2,0:T(2,128)S(1)} %add_bitcast_fusion), channel_id=1, replica_groups=mesh['dp'=8,'tensor'=4] {'tensor'}, dimensions={0}, use_global_device_ids=true | all-gather | bytes 2560 | tf_op jit(solution)/shard_map/all_gather | solution.py:48
  30.9 0.1 reshape.56
  31.0 0.0 collective-permute-done.1
  31.0 0.0 collective-permute-start.2
  31.0 6.7 %collective-permute-done.2 = bf16[64,1024]{1,0:T(8,128)(2,1)S(1)} collective-permute-done((bf16[64,1024]{1,0:T(8,128)(2,1)S(1)}, bf16[64,1024]{1,0:T(8,128)(2,1)S(1)}, u32[]{:S(2)}, u32[]{:S(2)}) %collective-permute-start.2) | collective-permute-done | bytes 131104 | tf_op jit(solution)/shard_map/ppermute | solution.py:33
  37.8 0.0 copy-done
  37.9 0.0 copy-start.1
  37.9 0.0 copy-start.3
  37.9 11.3 %all-gather.4.cloned.1.call-done = bf16[1024,2,1024]{2,0,1:T(8,128)(2,1)} async-done(((bf16[128,2,1024]{2,0,1:T(8,128)(2,1)}), bf16[1024,2,1024]{2,0,1:T(8,128)(2,1)}) %all-gather.4.cloned.1.call-update) | async-done | bytes 4194320 | tf_op jit(solution)/shard_map/all_gather | solution.py:41
  49.2 6.2 %copy.22 = bf16[1024,2,1024]{0,2,1:T(8,128)(2,1)} copy(bf16[1024,2,1024]{2,0,1:T(8,128)(2,1)} %all-gather.4.cloned.1.call-done) | data formatting | bytes 8388608 | tf_op jit(solution)/shard_map/all_gather | solution.py:41
  55.4 0.0 copy-done.1
  55.4 0.0 copy-done.3
  55.4 3.6 %fusion.2 = (f32[256,2]{0,1:T(2,128)S(1)}, f32[256,2,1024]{2,0,1:T(8,128)S(1)}) fusion(f32[2,1024]{1,0:T(2,128)S(1)} %convert_element_type.35, f32[2,1024]{1,0:T(2,128)S(1)} %copy-done.3, bf16[1024,2,1024]{0,2,1:T(8,128)(2,1)} %copy.22, bf16[512,1024]{1,0:T(8,128)(2,1)S(1)} %constant_dynamic-update-slice_fusion, s32[]{:T(128)S(6)} %select_n.33), kind=kOutput, calls=%fused_computation.4 | convolution fusion | flops 1076887040 | bytes 6834180 | tf_op jit(solution)/shard_map/dot_general | solution.py:43
  59.0 11.7 %psum.7 = f32[256,2]{0,1:T(2,128)S(1)} all-reduce(f32[256,2]{0,1:T(2,128)S(1)} %get-tuple-element.44), channel_id=1, replica_groups=mesh['dp'=8,'tensor'=4] {'tensor'}, use_global_device_ids=true, to_apply=%region_1.2 | all-reduce | flops 512 | bytes 4096 | tf_op jit(solution)/shard_map/psum | solution.py:47
  70.7 0.4 fusion.7
  71.1 0.8 convert_reduce_fusion
  72.0 0.0 copy-start.2
  72.0 0.5 copy.23
  72.5 0.7 copy-done.2
  73.2 4.5 %fusion.5 = f32[1024,2,1024]{2,0,1:T(8,128)} fusion(bf16[256,2,1024]{0,2,1:T(8,128)(2,1)S(1)} %copy.23, bf16[512,1024]{1,0:T(8,128)(2,1)S(1)} %copy-done.2, s32[]{:T(128)S(6)} %select_n.33), kind=kOutput, calls=%fused_computation.13 | convolution fusion | flops 1073741824 | bytes 9961476 | tf_op jit(solution)/shard_map/dot_general | solution.py:60
  77.7 0.0 reduce-scatter.5.cloned.1.call-update
  77.7 0.0 copy-start.4
  77.8 0.0 reduce-scatter.3.cloned.1.call-start
  77.8 4.3 %fusion.4 = bf16[256,1024]{1,0:T(8,128)(2,1)} fusion(bf16[1024,2,1024]{2,0,1:T(8,128)(2,1)} %all-gather.4.cloned.1.call-done, f32[256,2]{0,1:T(2,128)S(1)} %pad_add_fusion, f32[2,1024]{1,0:T(2,128)S(1)} %convert_element_type.35, u8[256,1024]{1,0:T(8,128)(4,1)S(1)} %fusion.7), kind=kOutput, calls=%fused_computation.12 | convolution fusion | flops 1077673984 | bytes 4990976 | tf_op jit(solution)/shard_map/dot_general | solution.py:54
  82.1 0.0 reduce-scatter.3.cloned.1.call-update
  82.1 0.0 copy-done.4
  82.1 0.6 dynamic-slice
  83.4 22.7 %all-reduce.2 = f32[4096]{0:T(1024)S(1)} all-reduce(f32[4096]{0:T(1024)S(1)} %bitcast.48), channel_id=4, replica_groups=mesh['dp'=8,'tensor'=4] {'dp'}, use_global_device_ids=true, to_apply=%region_6.8.clone | all-reduce | flops 4096 | bytes 32768
  106.1 0.1 dynamic-slice.1
  106.1 9.0 %all-gather.1 = f32[8,1,512]{2,1,0:T(1,128)S(1)} all-gather(f32[1,1,512]{2,1,0:T(1,128)S(1)} %bitcast.49), channel_id=1, replica_groups=mesh['dp'=8,'tensor'=4] {'dp'}, dimensions={0}, use_global_device_ids=true | all-gather | bytes 18432 | tf_op jit(solution)/shard_map/all_gather | solution.py:73
  115.2 0.1 fusion.12
  115.2 0.6 mul.150
  115.8 0.6 mul.152
  116.5 0.6 dynamic_slice.8
  117.0 29.5 %reduce-scatter.5.cloned.1.call-done = f32[128,2,1024]{2,0,1:T(8,128)} async-done(((f32[1024,2,1024]{2,0,1:T(8,128)}), f32[128,2,1024]{2,0,1:T(8,128)}) %reduce-scatter.5.cloned.1.call-update) | async-done | bytes 1048592 | tf_op jit(solution)/shard_map/reduce_scatter | solution.py:59
  146.6 1.3 broadcast_multiply_fusion
  147.9 1.8 %copy.25 = f32[128,2,1024]{2,1,0:T(2,128)} copy(f32[128,2,1024]{2,0,1:T(8,128)S(1)} %broadcast_multiply_fusion) | data formatting | bytes 2097152
  149.7 21.6 %reduce-scatter.3.cloned.1.call-done = bf16[64,1024]{1,0:T(8,128)(2,1)} async-done(((bf16[256,1024]{1,0:T(8,128)(2,1)}), bf16[64,1024]{1,0:T(8,128)(2,1)}) %reduce-scatter.3.cloned.1.call-update) | async-done | bytes 131088 | tf_op jit(solution)/shard_map/reduce_scatter | solution.py:55
  (15 shorter events, 0.2 us)
Async XLA Ops:
  7.2 30.6 %copy-start = (bf16[64,1024]{1,0:T(8,128)(2,1)S(1)}, bf16[64,1024]{1,0:T(8,128)(2,1)}, u32[]{:S(2)}) copy-start(bf16[64,1024]{1,0:T(8,128)(2,1)} %param.7) | copy-start | bytes 393220
  7.2 42.1 %all-gather.4.cloned.1.call-start = ((), (), s32[]{:S(2)}) async-start(), calls=%async_computation.2 | async-start | bytes 4718592 | tf_op jit(solution)/shard_map/all_gather | solution.py:41
  9.2 137.3 %reduce-scatter.5.cloned.1.call-start = ((), (), s32[]{:S(2)}) async-start(), calls=%async_computation.4 | async-start | bytes 9437184 | tf_op jit(solution)/shard_map/reduce_scatter | solution.py:59
  9.3 8.8 %collective-permute-start = (bf16[64,1024]{1,0:T(8,128)(2,1)}, bf16[64,1024]{1,0:T(8,128)(2,1)S(1)}, u32[]{:S(2)}, u32[]{:S(2)}) collective-permute-start(bf16[64,1024]{1,0:T(8,128)(2,1)} %param.7), channel_id=1, source_target_pairs={{0,1},{1,2},{2,3},{3,0},{4,5},{5,6},{6,7},{7,4},{8,9},{9,10},{10,1... | collective-permute-start | bytes 393224 | tf_op jit(solution)/shard_map/ppermute | solution.py:33
  18.1 12.9 %collective-permute-start.1 = (bf16[64,1024]{1,0:T(8,128)(2,1)S(1)}, bf16[64,1024]{1,0:T(8,128)(2,1)S(1)}, u32[]{:S(2)}, u32[]{:S(2)}) collective-permute-start(bf16[64,1024]{1,0:T(8,128)(2,1)S(1)} %collective-permute-done), channel_id=1, source_target_pairs={{0,1},{1,2},{2,3},{3,0},{4,5},{5,6},{6,7},{7,4},{8,9},{9,10},{10,1... | collective-permute-start | bytes 393224 | tf_op jit(solution)/shard_map/ppermute | solution.py:33
  31.0 6.8 %collective-permute-start.2 = (bf16[64,1024]{1,0:T(8,128)(2,1)S(1)}, bf16[64,1024]{1,0:T(8,128)(2,1)S(1)}, u32[]{:S(2)}, u32[]{:S(2)}) collective-permute-start(bf16[64,1024]{1,0:T(8,128)(2,1)S(1)} %collective-permute-done.1), channel_id=1, source_target_pairs={{0,1},{1,2},{2,3},{3,0},{4,5},{5,6},{6,7},{7,4},{8,9},{9,10},{10,1... | collective-permute-start | bytes 393224 | tf_op jit(solution)/shard_map/ppermute | solution.py:33
  37.9 17.5 %copy-start.1 = (bf16[512,1024]{1,0:T(8,128)(2,1)}, bf16[512,1024]{1,0:T(8,128)(2,1)S(1)}, u32[]{:S(2)}) copy-start(bf16[512,1024]{1,0:T(8,128)(2,1)S(1)} %constant_dynamic-update-slice_fusion) | copy-start | bytes 3145732
  37.9 17.5 %copy-start.3 = (f32[2,1024]{1,0:T(2,128)S(1)}, f32[2,1024]{1,0:T(2,128)}, u32[]{:S(2)}) copy-start(f32[2,1024]{1,0:T(2,128)} %param.11) | copy-start | bytes 24580
  72.0 1.2 copy-start.2
  77.7 4.4 %copy-start.4 = (u32[32]{0:T(128)S(1)}, u32[32]{0:T(128)}, u32[]{:S(2)}) copy-start(u32[32]{0:T(128)} %constant.54) | copy-start | bytes 388
  77.8 93.5 %reduce-scatter.3.cloned.1.call-start = ((), (), s32[]{:S(2)}) async-start(), calls=%async_computation.3 | async-start | bytes 655360 | tf_op jit(solution)/shard_map/reduce_scatter | solution.py:55
Sparse Core Ops, SparseCore 0:
  9.9 39.2 all-gather.3
  77.9 68.6 reduce-scatter.4
  149.4 21.8 reduce-scatter.2
